TPU v7x, 32 devices: a whole 2x2x4 slice. The times are simulated.
32 devices in a mesh: tissue: 2 (over core), row: 4 (over y, x), col: 4 (over z).
Axes of the slice: x: 2, y: 2, z: 4, core: 2. Of those that a mesh axis runs over, the one named last changes fastest.
Arguments:
- expr: float32 [1200, 16384], P(('tissue', 'row'), 'col'), parts along dimension 0, may hold values from -48 to 88
- win_genes: int32 [256], replicated, may hold values from 0 to 16383, as said below
Outputs:
- margin: float32 [512, 16384], P(('tissue', 'row'), 'col'), parts along dimension 0
- degree: float32 [32768], P(('tissue', 'col')), parts along dimension 0
There are 2 independent parts, one for each index of `tissue`. A program takes and returns all parts, laid end to end along the dimension named above; an argument that names none is the same for every part. Nothing has to cross between parts.
Inputs may be any that keep to these rules, and one draw needn't show every extreme that they name: `win_genes`: 256 distinct gene numbers.
All inputs are finite; a program needn't handle non-finite values.
Results may differ from a plain program's by a relative error of at most 0.00077.
Values may be sent and summed in bfloat16 or wider, within the bound.
A program may use at most 128 MiB of HBM per device.

v0:
```python
import functools

import jax
import jax.numpy as jnp
from jax import lax
from jax.experimental import pallas as pl
from jax.experimental.pallas import tpu as pltpu
from jax.sharding import PartitionSpec as P

MESH = pl.DeviceIdType.MESH
F32 = jnp.float32
BF16 = jnp.bfloat16


def power_eight(corr):
    half = (1.0 + corr) * 0.5
    half = half * half
    half = half * half
    return half * half


def flip(r, d):
    out = r
    for b in range(6):
        bit = 1 << b
        out = out + ((d // bit) % 2) * (1 - 2 * ((r // bit) % 2)) * bit
    return out


def dot(a, b, dims=((1,), (0,))):
    return lax.dot_general(a, b, (dims, ((), ())), preferred_element_type=F32)


def kernel(R, C, eps, expr, win, out, dego,
           stats, zl, zcol, zrt, zw, zwr, zwt, pbuf, macc, rs, degb, degr,
           s_st, r_st, s_aa, r_aa, s_ga, r_ga, s_zc, r_zc, s_zr, r_zr,
           s_up, r_up, s_dn, r_dn, s_rs, r_rs, s_dg, r_dg):
    r = lax.axis_index("row")
    c = lax.axis_index("col")
    S, width = expr.shape
    pad = zl.shape[0]
    slab = width // R
    W = zw.shape[2]
    per = W // R
    NC, chunk = zrt.shape[1], zrt.shape[2]

    barrier = pltpu.get_barrier_semaphore()
    for d in range(1, R):
        pl.semaphore_signal(barrier, inc=1, device_id={"row": flip(r, d)}, device_id_type=MESH)
    for d in range(1, C):
        pl.semaphore_signal(barrier, inc=1, device_id={"col": lax.rem(c + d, C)}, device_id_type=MESH)

    for j in range(R):
        cols = slice(j * slab, (j + 1) * slab)
        x = expr[:, cols]
        total = jnp.sum(x, axis=0, keepdims=True)
        dev = x - total * (1.0 / S)
        stats[0, 0:1, cols] = total
        stats[0, 1:2, cols] = jnp.sum(dev * dev, axis=0, keepdims=True)
    pl.semaphore_wait(barrier, R + C - 2)

    def rowcopy(src, dst, ss, rr, d):
        return pltpu.make_async_remote_copy(
            src_ref=src, dst_ref=dst, send_sem=ss, recv_sem=rr,
            device_id={"row": flip(r, d)}, device_id_type=MESH)

    def colcopy(src, dst, ss, rr, peer):
        return pltpu.make_async_remote_copy(
            src_ref=src, dst_ref=dst, send_sem=ss, recv_sem=rr,
            device_id={"col": peer}, device_id_type=MESH)

    st = [rowcopy(stats.at[0], stats.at[d], s_st.at[d], r_st.at[d], d) for d in range(1, R)]
    for cp in st:
        cp.start()
    macc[...] = jnp.zeros_like(macc)
    zl[pad - 16:pad, :] = jnp.zeros((16, width), BF16)
    pbuf[...] = jnp.ones_like(pbuf)
    for cp in st:
        cp.wait_recv()

    for j in range(R):
        cols = slice(j * slab, (j + 1) * slab)
        total = stats[0, 0:1, cols]
        for d in range(1, R):
            total = total + stats[d, 0:1, cols]
        mean = total / (S * R)
        sq = jnp.zeros_like(mean)
        for d in range(R):
            gap = stats[d, 0:1, cols] * (1.0 / S) - mean
            sq = sq + (stats[d, 1:2, cols] + S * gap * gap)
        inv = 1.0 / jnp.sqrt(sq + eps)
        zl[0:S, cols] = ((expr[:, cols] - mean) * inv).astype(BF16)

    mine = pl.ds(pl.multiple_of(r * pad, 16), pad)
    aa = []
    for k in range(NC):
        for d in range(1, R):
            q = flip(r, d)
            at = pl.multiple_of(q * slab + k * chunk, 128)
            aa.append(rowcopy(zl.at[:, pl.ds(at, chunk)],
                              zcol.at[q, mine, k * chunk:(k + 1) * chunk],
                              s_aa.at[k, d], r_aa.at[k, d], d))
            aa[-1].start()
    zcol[r, mine, :] = zl[:, pl.ds(pl.multiple_of(r * slab, 128), slab)]

    pick = jnp.zeros((pad, W), F32)
    for j in range(R):
        gene = lax.broadcasted_iota(jnp.int32, (slab, W), 0) + (c * width + j * slab)
        onehot = jnp.where(gene == win[...], 1.0, 0.0).astype(BF16)
        pick = pick + dot(zl[:, j * slab:(j + 1) * slab], onehot)
    zw[0] = pick.astype(BF16)
    zc = []
    for d in range(1, C):
        zc.append(colcopy(zw.at[0], zw.at[d], s_zc.at[d], r_zc.at[d], lax.rem(c + d, C)))
        zc[-1].start()

    zr_own = zcol.at[r]
    lo, hi = c > 0, c < C - 1

    def up(s, k):
        i = c - s
        return colcopy(zrt.at[i, k], zrt.at[i, k], s_up.at[s, k], r_up.at[s, k], c + 1)

    def up_in(s, k):
        i = c - s
        return colcopy(zrt.at[i, k], zrt.at[i, k], s_up.at[s - 1, k], r_up.at[s - 1, k], c + 1)

    def down(s, k):
        i = c + s
        return colcopy(zrt.at[i, k], zrt.at[i, k], s_dn.at[s, k], r_dn.at[s, k], c - 1)

    def down_in(s, k):
        i = c + s
        return colcopy(zrt.at[i, k], zrt.at[i, k], s_dn.at[s - 1, k], r_dn.at[s - 1, k], c - 1)

    for k in range(NC):
        for cp in aa[k * (R - 1):(k + 1) * (R - 1)]:
            cp.wait_recv()
        zrt[c, k] = zr_own[:, k * chunk:(k + 1) * chunk].T

        @pl.when(hi)
        def _():
            up(0, k).start()

        @pl.when(lo)
        def _():
            down(0, k).start()

    relay = R == 4

    def gather(k, d):
        piece = zcol.at[r, :, pl.ds(pl.multiple_of(k * chunk, 128), chunk)]
        return rowcopy(piece, piece, s_ga.at[k, d], r_ga.at[k, d], d)

    def forward(k, via, to):
        piece = zcol.at[flip(r, via), :, pl.ds(pl.multiple_of(k * chunk, 128), chunk)]
        return rowcopy(piece, piece, s_ga.at[k, R - 1], r_ga.at[k, R - 1], to)

    direct = R - 1 if relay else R
    for d in range(1, direct):
        gather(0, d).start()

    tot = zw[0].astype(F32)
    for cp in zc:
        cp.wait_recv()
    for d in range(1, C):
        tot = tot + zw[d].astype(F32)
    zwr[0] = tot.astype(BF16)
    zr = []
    for d in range(1, R):
        zr.append(rowcopy(zwr.at[0], zwr.at[d], s_zr.at[d], r_zr.at[d], d))
        zr[-1].start()
    for k in range(1, NC):
        for d in range(1, direct):
            gather(k, d).start()
    for cp in zr:
        cp.wait_recv()
    for d in range(R):
        zwt[pl.ds(pl.multiple_of(flip(r, d) * pad, 16), pad), :] = zwr[d]

    def compute(i, k, d_lo, d_hi):
        def one(d, _):
            j = flip(r, d)
            adj = power_eight(dot(zrt[i, k], zcol[j])).astype(BF16)
            macc[j] += dot(pbuf[i, k], adj)
            return 0
        lax.fori_loop(d_lo, d_hi, one, 0)

    def panel(i, k):
        pt = power_eight(dot(zrt[i, k], zwt[...])).T
        pbuf[i, k, 0:W, :] = pt.astype(BF16)

    def arrive(s, k):
        @pl.when(c - s >= 0)
        def _():
            up_in(s, k).wait_recv()

            @pl.when(hi)
            def _():
                up(s, k).start()

        @pl.when(c + s < C)
        def _():
            down_in(s, k).wait_recv()

            @pl.when(lo)
            def _():
                down(s, k).start()

    def phase(s, t_lo, t_hi, start, d_hi):
        def step(k, _):
            arrive(s, k)

            def each(t, _):
                i = c + (1 - 2 * (t % 2)) * ((t + 1) // 2)

                @pl.when((i >= 0) & (i < C))
                def _():
                    @pl.when(start(t) == 0)
                    def _():
                        panel(i, k)
                    compute(i, k, start(t), d_hi)
                return 0
            lax.fori_loop(t_lo, t_hi, each, 0)
            return 0
        lax.fori_loop(0, NC, step, 0)

    def own(k, _):
        panel(c, k)
        compute(c, k, 0, 1)
        return 0
    lax.fori_loop(0, NC, own, 0)

    for k in range(NC):
        arrive(1, k)
        for d in range(1, R - 1):
            gather(k, d).wait_recv()
        if relay:
            via = 1 if k < NC // 2 else 2
            forward(k, via, 3 - via).start()
    phase(2, 0, 3, lambda t: jnp.where(t == 0, 1, 0), R - 1)
    for k in range(NC):
        gather(k, R - 1).wait_recv()
    phase(3, 0, 7, lambda t: jnp.where(t < 3, R - 1, 0), R)
    if C > 4:
        def later(s, _):
            phase(s, 2 * s - 1, 2 * s + 1, lambda t: 0, R)
            return 0
        lax.fori_loop(4, C, later, 0)

    out_cp = []
    for d in range(1, R):
        q = pl.multiple_of(flip(r, d) * per, 8)
        for j in range(R):
            out_cp.append(rowcopy(macc.at[j, pl.ds(q, per), :], rs.at[d, j],
                                  s_rs.at[d, j], r_rs.at[d, j], d))
            out_cp[-1].start()
    for j in range(R):
        degb[j] = macc[j, W:W + 1, :]
    zs = zcol[r].astype(F32)
    self_term = power_eight(jnp.sum(zs * zs, axis=0, keepdims=True))
    degb[r] = degb[r] - self_term.astype(BF16).astype(F32)
    dg = []
    for d in range(1, R):
        dg.append(rowcopy(degb, degr.at[d], s_dg.at[d], r_dg.at[d], d))
        dg[-1].start()
    own_rows = pl.ds(pl.multiple_of(r * per, 8), per)
    for j in range(R):
        total = macc[j, own_rows, :]
        for d in range(1, R):
            out_cp[(d - 1) * R + j].wait_recv()
            total = total + rs[d, j]
        out[:, j * slab:(j + 1) * slab] = total
    for cp in dg:
        cp.wait_recv()
    for j in range(R):
        total = degb[j]
        for d in range(1, R):
            total = total + degr[d, j]
        dego[:, j * slab:(j + 1) * slab] = total

    for cp in st + aa + zc + zr + out_cp + dg:
        cp.wait_send()
    for k in range(NC):
        for d in range(1, R):
            gather(k, d).wait_send()

    def drain(s, _):
        def each(k, _):
            @pl.when(hi & (c - s >= 0))
            def _():
                up(s, k).wait_send()

            @pl.when(lo & (c + s < C))
            def _():
                down(s, k).wait_send()
            return 0
        lax.fori_loop(0, NC, each, 0)
        return 0
    lax.fori_loop(0, C - 1, drain, 0)


def solution(mesh):
    R, C = mesh.shape["row"], mesh.shape["col"]

    def body(expr, win):
        S, width = expr.shape
        W = win.shape[0]
        pad = (S + 15) // 16 * 16
        slab = width // R
        chunk = min(256, slab)
        NC = slab // chunk
        V = pltpu.VMEM
        dma = pltpu.SemaphoreType.DMA
        vm = pl.BlockSpec(memory_space=pltpu.VMEM)
        margin, degree = pl.pallas_call(
            functools.partial(kernel, R, C, 1e-6),
            out_shape=(jax.ShapeDtypeStruct((W // R, width), F32),
                       jax.ShapeDtypeStruct((1, width), F32)),
            in_specs=[vm, vm],
            out_specs=(vm, vm),
            scratch_shapes=[
                V((R, 2, width), F32),
                V((pad, width), BF16),
                V((R, R * pad, slab), BF16),
                V((C, NC, chunk, R * pad), BF16),
                V((C, pad, W), BF16),
                V((R, pad, W), BF16),
                V((R * pad, W), BF16),
                V((C, NC, W + 16, chunk), BF16),
                V((R, W + 16, slab), F32),
                V((R, R, W // R, slab), F32),
                V((R, 1, slab), F32),
                V((R, R, 1, slab), F32),
                dma((R,)), dma((R,)), dma((NC, R)), dma((NC, R)), dma((NC, R)), dma((NC, R)),
                dma((C,)), dma((C,)), dma((R,)), dma((R,)),
                dma((C, NC)), dma((C, NC)), dma((C, NC)), dma((C, NC)),
                dma((R, R)), dma((R, R)), dma((R,)), dma((R,)),
            ],
            compiler_params=pltpu.CompilerParams(
                collective_id=0, has_side_effects=True, vmem_limit_bytes=56 << 20),
        )(expr, win.reshape(1, W))
        return margin, degree.reshape(width)

    in_specs = (P(("tissue", "row"), "col"), P())
    out_specs = (P(("tissue", "row"), "col"), P(("tissue", "col")))
    return jax.shard_map(body, mesh=mesh, in_specs=in_specs, out_specs=out_specs, check_vma=False)
```

profile of v0, /device:TPU:0, one launch (start us, length us, event | category | flops | bytes accessed | tf_op | source)
XLA Modules:
  0.0 171.2 jit_solution(12129117435905630273)
XLA Ops:
  0.6 167.0 %shard_map.41 = (f32[64,4096]{1,0:T(8,128)}, f32[1,4096]{1,0:T(1,128)}) custom-call(f32[150,4096]{1,0:T(8,128)} %expr.1, s32[1,256]{1,0:T(1,128)} %bitcast.3), custom_call_target="tpu_custom_call" | custom-call | tf_op jit(solution)/shard_map/pallas_call | solution.py:316
  167.6 2.3 %copy.6 = f32[64,4096]{1,0:T(8,128)} copy(f32[64,4096]{1,0:T(8,128)} %get-tuple-element.8) | data formatting | bytes 2097152
  169.9 1.3 copy.7
where the time goes:
time: 171 us
  Pallas kernels  167 us (98%)
  local copies, waits for them, and re-layouts  3.59 us (2%)
    pallas_call x1, Pallas kernels, body(): pl.pallas_call(functools.partial(kernel, R, C, 1e-06), out_shape=(jax.Sha...  167 us
    unnamed x2, local copies, waits for them, and re-layouts  3.59 us

commit v1 on v0

--- a/solution.py
+++ b/solution.py
@@ -300,10 +300,458 @@
     lax.fori_loop(0, C - 1, drain, 0)
 
 
+LIMIT = 65535.0
+
+
+def quantize(v):
+    h = v.shape[0] // 2
+    top = jnp.maximum(jnp.max(v, axis=0, keepdims=True), 1e-20)
+    inv = LIMIT / top
+    code = (v * inv + 0.5).astype(jnp.int32)
+    return code[:h] | lax.shift_left(code[h:], 16), top
+
+
+def restore(code, top):
+    unit = top * (1.0 / LIMIT)
+    low = (code & 65535).astype(F32) * unit
+    high = lax.shift_right_logical(code, 16).astype(F32) * unit
+    return low, high
+
+
+def gather_plan():
+    plan = {}
+    for d in (1, 2):
+        e, sent, groups = d - 1, set(), []
+        for m in range(4):
+            group = []
+            for piece in [(3 ^ m, e), (d ^ m, e), (d ^ m, 1 - e)]:
+                if piece not in sent:
+                    sent.add(piece)
+                    group.append(piece)
+            groups.append(group)
+        plan[d] = groups
+    return plan
+
+
+def folded_kernel(eps, expr, win, out, dego,
+                  stats, zcol, zf, zt, zw, zwr, zwt, zwn, pcol, prow, macc, ret,
+                  rtq, rta, rbq, rba, rsq, rsa, rbufq, rbufa, degb, degr,
+                  s_st, r_st, s_ag, r_ag, s_rl, s_z, r_z, s_zf, s_zc, r_zc, s_zr, r_zr,
+                  s_rt, r_rt, s_rs, r_rs, s_dg, r_dg):
+    R, C = 4, 4
+    t = lax.axis_index("tissue")
+    r = lax.axis_index("row")
+    c = lax.axis_index("col")
+    p = c + t * (C - 1 - 2 * c)
+    S, width = expr.shape
+    slab = width // R
+    half = slab // 2
+    pad = zcol.shape[1] // R
+    W = zw.shape[2]
+    per = W // R
+    CH = zt.shape[1] // 2
+
+    def rowpeer(d):
+        return {"row": flip(r, d)}
+
+    def colpeer(q):
+        return {"col": q + t * (C - 1 - 2 * q)}
+
+    def copy(src, dst, ss, rr, dev):
+        return pltpu.make_async_remote_copy(
+            src_ref=src, dst_ref=dst, send_sem=ss, recv_sem=rr,
+            device_id=dev, device_id_type=MESH)
+
+    started = []
+
+    def send(src, dst, ss, rr, dev):
+        cp = copy(src, dst, ss, rr, dev)
+        cp.start()
+        started.append(cp)
+
+    def arrived(dst, rr):
+        copy(dst, dst, rr, rr, rowpeer(1)).wait_recv()
+
+    barrier = pltpu.get_barrier_semaphore()
+    for d in range(1, R):
+        pl.semaphore_signal(barrier, inc=1, device_id=rowpeer(d), device_id_type=MESH)
+    for d in range(1, C):
+        pl.semaphore_signal(barrier, inc=1, device_id={"col": lax.rem(c + d, C)}, device_id_type=MESH)
+
+    def at(m):
+        return pl.ds(pl.multiple_of(flip(r, m) * slab, 128), slab)
+
+    for j in range(R):
+        cols = slice(j * slab, (j + 1) * slab)
+        x = expr[:, cols]
+        total = jnp.sum(x, axis=0, keepdims=True)
+        dev = x - total * (1.0 / S)
+        stats[0, 0:1, cols] = total
+        stats[0, 1:2, cols] = jnp.sum(dev * dev, axis=0, keepdims=True)
+    pl.semaphore_wait(barrier, R + C - 2)
+    for d in range(1, R):
+        send(stats.at[0], stats.at[d], s_st.at[d], r_st.at[d], rowpeer(d))
+    for m in range(R):
+        zcol[m, pad - 16:pad, :] = jnp.zeros((16, slab), BF16)
+        macc[m] = jnp.zeros(macc.shape[1:], F32)
+        pcol[m, W:, :] = jnp.ones((16, slab), BF16)
+    for f in range(2):
+        prow[f, W:, :] = jnp.ones((16, slab), BF16)
+        ret[f] = jnp.zeros(ret.shape[1:], F32)
+    for d in range(1, R):
+        arrived(stats.at[d], r_st.at[d])
+
+    plan = gather_plan()
+
+    def direct(d, g):
+        for rel, e in plan[d][g]:
+            cols = slice(e * half, (e + 1) * half)
+            send(zcol.at[rel, 0:pad, cols], zcol.at[rel ^ d, d * pad:(d + 1) * pad, cols],
+                 s_ag.at[d, rel, e], r_ag.at[d, rel ^ d, e], rowpeer(d))
+
+    seen = set()
+
+    def landed(d, m, e):
+        if (d, m, e) in seen:
+            return
+        seen.add((d, m, e))
+        cols = slice(e * half, (e + 1) * half)
+        arrived(zcol.at[m, d * pad:(d + 1) * pad, cols], r_ag.at[d, m, e])
+
+    def relay(g):
+        for d in (1, 2):
+            n, e = 3 - d, 2 - d
+            rel = d ^ g
+            cols = slice(e * half, (e + 1) * half)
+            piece = zcol.at[rel, n * pad:(n + 1) * pad, cols]
+            landed(n, rel, e)
+            send(piece, zcol.at[g, 3 * pad:4 * pad, cols],
+                 s_rl.at[d, g], r_ag.at[3, g, e], rowpeer(d))
+
+    def gathered(m):
+        for d in range(1, R):
+            for e in range(2):
+                landed(d, m, e)
+
+    for m in (3, 1, 2, 0):
+        cols = at(m)
+        total = stats[0, 0:1, cols]
+        for d in range(1, R):
+            total = total + stats[d, 0:1, cols]
+        mean = total / (S * R)
+        sq = jnp.zeros_like(mean)
+        for d in range(R):
+            gap = stats[d, 0:1, cols] * (1.0 / S) - mean
+            sq = sq + (stats[d, 1:2, cols] + S * gap * gap)
+        inv = 1.0 / jnp.sqrt(sq + eps)
+        zcol[m, 0:S, :] = ((expr[:, cols] - mean) * inv).astype(BF16)
+        if m == 2:
+            for d in (1, 2):
+                direct(d, 0)
+
+    zslot = p // 3
+    zpeer = colpeer(jnp.where(p == 3, 1, p + 1))
+
+    def zsend(d):
+        rows = slice(d * pad, (d + 1) * pad)
+        send(zcol.at[0, rows, :], zf.at[zslot, rows, :], s_z.at[d], r_z.at[zslot, d], zpeer)
+
+    zsend(0)
+
+    pick = jnp.zeros((pad, W), F32)
+    for m in range(R):
+        gene = lax.broadcasted_iota(jnp.int32, (slab, W), 0) + (c * width + flip(r, m) * slab)
+        onehot = jnp.where(gene == win[...], 1.0, 0.0).astype(BF16)
+        pick = pick + dot(zcol[m, 0:pad, :], onehot)
+    zw[0] = pick.astype(BF16)
+    for d in range(1, C):
+        send(zw.at[0], zw.at[d], s_zc.at[d], r_zc.at[d], {"col": lax.rem(c + d, C)})
+
+    relay(0)
+    tot = zw[0].astype(F32)
+    for d in range(1, C):
+        arrived(zw.at[d], r_zc.at[d])
+        tot = tot + zw[d].astype(F32)
+    zwr[0] = tot.astype(BF16)
+    for d in range(1, R):
+        send(zwr.at[0], zwr.at[d], s_zr.at[d], r_zr.at[d], rowpeer(d))
+    for d in (1, 2):
+        direct(d, 1)
+    for d in range(1, R):
+        for e in range(2):
+            landed(d, 0, e)
+        zsend(d)
+
+    zt[0] = zcol[0].T
+    for d in range(1, R):
+        arrived(zwr.at[d], r_zr.at[d])
+    for d in range(R):
+        zwt[d * pad:(d + 1) * pad, :] = zwr[d]
+    zwn[...] = zwt[...].T
+
+    def panel_col(m):
+        pcol[m, 0:W, :] = power_eight(dot(zwn[...], zcol[m])).astype(BF16)
+
+    def chunk(k):
+        return pl.ds(pl.multiple_of(k * CH, 128), CH)
+
+    def own(m):
+        def step(k, _):
+            rows = chunk(k)
+            adj = power_eight(dot(zt[0, rows, :], zcol[m])).astype(BF16)
+            macc[m] += dot(pcol[0, :, rows], adj)
+            return 0
+        lax.fori_loop(0, 2, step, 0)
+
+    def cross(f, k, m):
+        rows = chunk(k)
+        adj = power_eight(dot(zt[1 + f, rows, :], zcol[m])).astype(BF16)
+        macc[m] += dot(prow[f, :, rows], adj)
+        ret[f, :, rows] += dot(pcol[m], adj, ((1,), (1,)))
+
+    def crosses(f, m_lo, m_hi):
+        def step(i, _):
+            cross(f, lax.rem(i, 2), m_lo + i // 2)
+            return 0
+        lax.fori_loop(0, 2 * (m_hi - m_lo), step, 0)
+
+    def prepare(f, known):
+        for d in range(R):
+            if d not in known:
+                arrived(zf.at[f, d * pad:(d + 1) * pad, :], r_z.at[f, d])
+        zt[1 + f] = zf[f].T
+        prow[f, 0:W, :] = power_eight(dot(zwn[...], zf[f])).astype(BF16)
+
+    def zcopy(f, d):
+        rows = slice(d * pad, (d + 1) * pad)
+        dest = 2 if f == 0 else 0
+        return copy(zf.at[f, rows, :], zf.at[1, rows, :], s_zf.at[f, d], r_z.at[1, d], colpeer(dest))
+
+    def zrelay(f, ds):
+        @pl.when(p == 1)
+        def _():
+            for d in ds:
+                arrived(zf.at[f, d * pad:(d + 1) * pad, :], r_z.at[f, d])
+                zcopy(f, d).start()
+
+    def retcopy(f, k):
+        cols = slice(k * CH, (k + 1) * CH)
+        if f == 0:
+            dest, slot = p - 1, 0
+        else:
+            dest = jnp.where(p == 2, 0, 3)
+            slot = (p + 1) // 2
+        return [copy(rtq.at[f, :, cols], rbq.at[slot, :, cols], s_rt.at[f, k, 0], r_rt.at[slot, k, 0], colpeer(dest)),
+                copy(rta.at[f, k], rba.at[slot, k], s_rt.at[f, k, 1], r_rt.at[slot, k, 1], colpeer(dest))]
+
+    def give_back(f, k):
+        cols = slice(k * CH, (k + 1) * CH)
+        code, top = quantize(ret[f, 0:W, cols])
+        rtq[f, :, cols] = code
+        rta[f, k, 0:1, :] = top
+        rta[f, k, 1:2, :] = ret[f, W:W + 1, cols]
+        for cp in retcopy(f, k):
+            cp.start()
+
+    def take_back(slot):
+        for k in range(2):
+            cols = slice(k * CH, (k + 1) * CH)
+            arrived(rbq.at[slot, :, cols], r_rt.at[slot, k, 0])
+            arrived(rba.at[slot, k], r_rt.at[slot, k, 1])
+            low, high = restore(rbq[slot, :, cols], rba[slot, k, 0:1, :])
+            macc[0, 0:W // 2, cols] += low
+            macc[0, W // 2:W, cols] += high
+            macc[0, W:W + 1, cols] += rba[slot, k, 1:2, :]
+
+    def scatter(m):
+        for d in range(1, R):
+            rows = pl.ds(pl.multiple_of(flip(r, d) * per, 8), per)
+            code, top = quantize(macc[m, rows, :])
+            rsq[d, m] = code
+            rsa[d, m] = top
+            send(rsq.at[d, m], rbufq.at[d, m ^ d], s_rs.at[d, m, 0], r_rs.at[d, m ^ d, 0], rowpeer(d))
+            send(rsa.at[d, m], rbufa.at[d, m ^ d], s_rs.at[d, m, 1], r_rs.at[d, m ^ d, 1], rowpeer(d))
+
+    early, late = p >= 1, p <= 2
+
+    panel_col(0)
+    own(0)
+    relay(1)
+    for d in (1, 2):
+        direct(d, 2)
+        direct(d, 3)
+    zrelay(0, (0, 1))
+    gathered(1)
+    panel_col(1)
+    own(1)
+    relay(2)
+    zrelay(0, (2, 3))
+    zrelay(1, (0, 1))
+
+    @pl.when(p == 1)
+    def _():
+        prepare(0, range(R))
+
+    @pl.when(p >= 2)
+    def _():
+        prepare(0, ())
+
+    @pl.when(early)
+    def _():
+        crosses(0, 0, 2)
+    relay(3)
+    gathered(2)
+    panel_col(2)
+    own(2)
+    zrelay(1, (2, 3))
+
+    @pl.when(early)
+    def _():
+        crosses(0, 2, 3)
+    gathered(3)
+    panel_col(3)
+    own(3)
+
+    @pl.when(early)
+    def _():
+        crosses(0, 3, 4)
+        for k in range(2):
+            give_back(0, k)
+
+    @pl.when(p == 1)
+    def _():
+        prepare(1, range(R))
+
+    @pl.when((p == 0) | (p == 2))
+    def _():
+        prepare(1, ())
+
+    for k in range(2):
+        @pl.when(late)
+        def _():
+            def step(m, _):
+                cross(1, k, m)
+                return 0
+            lax.fori_loop(0, R, step, 0)
+            give_back(1, k)
+    for m in range(1, R):
+        scatter(m)
+    take_back(0)
+
+    @pl.when((p == 0) | (p == 3))
+    def _():
+        take_back(1)
+
+    zs = zcol[0].astype(F32)
+    self_term = power_eight(jnp.sum(zs * zs, axis=0, keepdims=True))
+    for m in range(R):
+        degb[m] = macc[m, W:W + 1, :]
+    degb[0] = degb[0] - self_term.astype(BF16).astype(F32)
+    for d in range(1, R):
+        send(degb, degr.at[d], s_dg.at[d], r_dg.at[d], rowpeer(d))
+    scatter(0)
+
+    hp = per // 2
+    mine = pl.multiple_of(r * per, 8)
+    for m in (1, 2, 3, 0):
+        for q in range(2):
+            acc = macc[m, pl.ds(mine + q * hp, hp), :]
+            for d in range(1, R):
+                if q == 0:
+                    arrived(rbufq.at[d, m], r_rs.at[d, m, 0])
+                    arrived(rbufa.at[d, m], r_rs.at[d, m, 1])
+                acc = acc + restore(rbufq[d, m], rbufa[d, m])[q]
+            out[q * hp:(q + 1) * hp, at(m)] = acc
+    for d in range(1, R):
+        arrived(degr.at[d], r_dg.at[d])
+    for m in range(R):
+        total = degb[m]
+        for d in range(1, R):
+            total = total + degr[d, m ^ d]
+        dego[:, at(m)] = total
+
+    for cp in started:
+        cp.wait_send()
+
+    @pl.when(p == 1)
+    def _():
+        for f in range(2):
+            for d in range(R):
+                zcopy(f, d).wait_send()
+
+    @pl.when(early)
+    def _():
+        for k in range(2):
+            for cp in retcopy(0, k):
+                cp.wait_send()
+
+    @pl.when(late)
+    def _():
+        for k in range(2):
+            for cp in retcopy(1, k):
+                cp.wait_send()
+
+
+def folded(expr, win):
+    R = C = 4
+    S, width = expr.shape
+    W = win.shape[0]
+    pad = (S + 15) // 16 * 16
+    slab = width // R
+    V = pltpu.VMEM
+    I32 = jnp.int32
+    dma = pltpu.SemaphoreType.DMA
+    vm = pl.BlockSpec(memory_space=pltpu.VMEM)
+    half = slab // 2
+    margin, degree = pl.pallas_call(
+        functools.partial(folded_kernel, 1e-6),
+        out_shape=(jax.ShapeDtypeStruct((W // R, width), F32),
+                   jax.ShapeDtypeStruct((1, width), F32)),
+        in_specs=[vm, vm],
+        out_specs=(vm, vm),
+        scratch_shapes=[
+            V((R, 2, width), F32),
+            V((R, R * pad, slab), BF16),
+            V((2, R * pad, slab), BF16),
+            V((3, slab, R * pad), BF16),
+            V((C, pad, W), BF16),
+            V((R, pad, W), BF16),
+            V((R * pad, W), BF16),
+            V((W, R * pad), BF16),
+            V((R, W + 16, slab), BF16),
+            V((2, W + 16, slab), BF16),
+            V((R, W + 16, slab), F32),
+            V((2, W + 16, slab), F32),
+            V((2, W // 2, slab), I32),
+            V((2, 2, 2, half), F32),
+            V((2, W // 2, slab), I32),
+            V((2, 2, 2, half), F32),
+            V((R, R, W // R // 2, slab), I32),
+            V((R, R, 1, slab), F32),
+            V((R, R, W // R // 2, slab), I32),
+            V((R, R, 1, slab), F32),
+            V((R, 1, slab), F32),
+            V((R, R, 1, slab), F32),
+            dma((R,)), dma((R,)),
+            dma((R, R, 2)), dma((R, R, 2)), dma((R, R)),
+            dma((R,)), dma((2, R)), dma((2, R)),
+            dma((C,)), dma((C,)), dma((R,)), dma((R,)),
+            dma((2, 2, 2)), dma((2, 2, 2)),
+            dma((R, R, 2)), dma((R, R, 2)),
+            dma((R,)), dma((R,)),
+        ],
+        compiler_params=pltpu.CompilerParams(
+            collective_id=0, has_side_effects=True, vmem_limit_bytes=60 << 20),
+    )(expr, win.reshape(1, W))
+    return margin, degree.reshape(width)
+
+
 def solution(mesh):
     R, C = mesh.shape["row"], mesh.shape["col"]
 
     def body(expr, win):
+        if R == 4 and C == 4:
+            return folded(expr, win)
         S, width = expr.shape
         W = win.shape[0]
         pad = (S + 15) // 16 * 16

time: 171 us -> 118 us (0.69)
  the two profiles are of different devices: /device:TPU:0 before, /device:TPU:13 now
where the time goes in v1:
time: 118 us
  Pallas kernels  114 us (97%)
  local copies, waits for them, and re-layouts  3.59 us (3%)
    pallas_call x1, Pallas kernels, folded(): pl.pallas_call(functools.partial(folded_kernel, 1e-06), out_shape=(jax.Sh...  114 us
    unnamed x2, local copies, waits for them, and re-layouts  3.59 us

profile of v1, /device:TPU:13, one launch (start us, length us, event | category | flops | bytes accessed | tf_op | source)
XLA Modules:
  0.0 118.1 jit_solution(2080088309378415189)
XLA Ops:
  0.6 113.9 %shard_map.41 = (f32[64,4096]{1,0:T(8,128)}, f32[1,4096]{1,0:T(1,128)}) custom-call(f32[150,4096]{1,0:T(8,128)} %expr.1, s32[1,256]{1,0:T(1,128)} %bitcast.3), custom_call_target="tpu_custom_call" | custom-call | tf_op jit(solution)/shard_map/pallas_call | solution.py:706
  114.5 2.3 %copy.6 = f32[64,4096]{1,0:T(8,128)} copy(f32[64,4096]{1,0:T(8,128)} %get-tuple-element.8) | data formatting | bytes 2097152
  116.8 1.3 %copy.7 = f32[4096]{0:T(1024)} copy(f32[4096]{0:T(1024)} %bitcast.2) | data formatting | bytes 32768

commit v2 on v1

--- a/solution.py
+++ b/solution.py
@@ -350,6 +350,10 @@
     W = zw.shape[2]
     per = W // R
     CH = zt.shape[1] // 2
+    full = (S + 7) // 8 * 8
+
+    def block(d):
+        return slice(d * pad, d * pad + full)
 
     def rowpeer(d):
         return {"row": flip(r, d)}
@@ -371,6 +375,13 @@
 
     def arrived(dst, rr):
         copy(dst, dst, rr, rr, rowpeer(1)).wait_recv()
+
+    for d in range(R):
+        tail = slice((d + 1) * pad - 16, (d + 1) * pad)
+        for m in range(R):
+            zcol[m, tail, :] = jnp.zeros((16, slab), BF16)
+        for f in range(2):
+            zf[f, tail, :] = jnp.zeros((16, slab), BF16)
 
     barrier = pltpu.get_barrier_semaphore()
     for d in range(1, R):
@@ -392,7 +403,6 @@
     for d in range(1, R):
         send(stats.at[0], stats.at[d], s_st.at[d], r_st.at[d], rowpeer(d))
     for m in range(R):
-        zcol[m, pad - 16:pad, :] = jnp.zeros((16, slab), BF16)
         macc[m] = jnp.zeros(macc.shape[1:], F32)
         pcol[m, W:, :] = jnp.ones((16, slab), BF16)
     for f in range(2):
@@ -406,7 +416,7 @@
     def direct(d, g):
         for rel, e in plan[d][g]:
             cols = slice(e * half, (e + 1) * half)
-            send(zcol.at[rel, 0:pad, cols], zcol.at[rel ^ d, d * pad:(d + 1) * pad, cols],
+            send(zcol.at[rel, block(0), cols], zcol.at[rel ^ d, block(d), cols],
                  s_ag.at[d, rel, e], r_ag.at[d, rel ^ d, e], rowpeer(d))
 
     seen = set()
@@ -416,16 +426,15 @@
             return
         seen.add((d, m, e))
         cols = slice(e * half, (e + 1) * half)
-        arrived(zcol.at[m, d * pad:(d + 1) * pad, cols], r_ag.at[d, m, e])
-
-    def relay(g):
-        for d in (1, 2):
+        arrived(zcol.at[m, block(d), cols], r_ag.at[d, m, e])
+
+    def relay(g, links=(1, 2)):
+        for d in links:
             n, e = 3 - d, 2 - d
             rel = d ^ g
             cols = slice(e * half, (e + 1) * half)
-            piece = zcol.at[rel, n * pad:(n + 1) * pad, cols]
             landed(n, rel, e)
-            send(piece, zcol.at[g, 3 * pad:4 * pad, cols],
+            send(zcol.at[rel, block(n), cols], zcol.at[g, block(3), cols],
                  s_rl.at[d, g], r_ag.at[3, g, e], rowpeer(d))
 
     def gathered(m):
@@ -453,10 +462,8 @@
     zpeer = colpeer(jnp.where(p == 3, 1, p + 1))
 
     def zsend(d):
-        rows = slice(d * pad, (d + 1) * pad)
+        rows = block(d)
         send(zcol.at[0, rows, :], zf.at[zslot, rows, :], s_z.at[d], r_z.at[zslot, d], zpeer)
-
-    zsend(0)
 
     pick = jnp.zeros((pad, W), F32)
     for m in range(R):
@@ -466,6 +473,7 @@
     zw[0] = pick.astype(BF16)
     for d in range(1, C):
         send(zw.at[0], zw.at[d], s_zc.at[d], r_zc.at[d], {"col": lax.rem(c + d, C)})
+    zsend(0)
 
     relay(0)
     tot = zw[0].astype(F32)
@@ -518,12 +526,12 @@
     def prepare(f, known):
         for d in range(R):
             if d not in known:
-                arrived(zf.at[f, d * pad:(d + 1) * pad, :], r_z.at[f, d])
+                arrived(zf.at[f, block(d), :], r_z.at[f, d])
         zt[1 + f] = zf[f].T
         prow[f, 0:W, :] = power_eight(dot(zwn[...], zf[f])).astype(BF16)
 
     def zcopy(f, d):
-        rows = slice(d * pad, (d + 1) * pad)
+        rows = block(d)
         dest = 2 if f == 0 else 0
         return copy(zf.at[f, rows, :], zf.at[1, rows, :], s_zf.at[f, d], r_z.at[1, d], colpeer(dest))
 
@@ -531,48 +539,69 @@
         @pl.when(p == 1)
         def _():
             for d in ds:
-                arrived(zf.at[f, d * pad:(d + 1) * pad, :], r_z.at[f, d])
+                arrived(zf.at[f, block(d), :], r_z.at[f, d])
                 zcopy(f, d).start()
 
-    def retcopy(f, k):
+    def back_copies(f, k):
         cols = slice(k * CH, (k + 1) * CH)
         if f == 0:
             dest, slot = p - 1, 0
         else:
             dest = jnp.where(p == 2, 0, 3)
             slot = (p + 1) // 2
-        return [copy(rtq.at[f, :, cols], rbq.at[slot, :, cols], s_rt.at[f, k, 0], r_rt.at[slot, k, 0], colpeer(dest)),
-                copy(rta.at[f, k], rba.at[slot, k], s_rt.at[f, k, 1], r_rt.at[slot, k, 1], colpeer(dest))]
+        made = []
+        for d in (3, 1, 2, 0):
+            dev = {**colpeer(dest), **(rowpeer(d) if d else {})}
+            made += [copy(rtq.at[f, d, :, cols], rbq.at[slot, d, :, cols],
+                          s_rt.at[f, k, d, 0], r_rt.at[slot, k, d, 0], dev),
+                     copy(rta.at[f, k, d], rba.at[slot, k, d],
+                          s_rt.at[f, k, d, 1], r_rt.at[slot, k, d, 1], dev)]
+        return made
 
     def give_back(f, k):
         cols = slice(k * CH, (k + 1) * CH)
-        code, top = quantize(ret[f, 0:W, cols])
-        rtq[f, :, cols] = code
-        rta[f, k, 0:1, :] = top
-        rta[f, k, 1:2, :] = ret[f, W:W + 1, cols]
-        for cp in retcopy(f, k):
-            cp.start()
+        made = back_copies(f, k)
+        for i, d in enumerate((3, 1, 2, 0)):
+            rows = pl.ds(pl.multiple_of(flip(r, d) * per, 8), per)
+            code, top = quantize(ret[f, rows, cols])
+            rtq[f, d, :, cols] = code
+            rta[f, k, d, 0:1, :] = top
+            rta[f, k, d, 1:2, :] = ret[f, W:W + 1, cols]
+            made[2 * i].start()
+            made[2 * i + 1].start()
 
     def take_back(slot):
         for k in range(2):
             cols = slice(k * CH, (k + 1) * CH)
-            arrived(rbq.at[slot, :, cols], r_rt.at[slot, k, 0])
-            arrived(rba.at[slot, k], r_rt.at[slot, k, 1])
-            low, high = restore(rbq[slot, :, cols], rba[slot, k, 0:1, :])
-            macc[0, 0:W // 2, cols] += low
-            macc[0, W // 2:W, cols] += high
-            macc[0, W:W + 1, cols] += rba[slot, k, 1:2, :]
+            for m in range(R):
+                arrived(rbq.at[slot, m, :, cols], r_rt.at[slot, k, m, 0])
+                arrived(rba.at[slot, k, m], r_rt.at[slot, k, m, 1])
+                there = pl.ds(pl.multiple_of(flip(r, m) * slab + k * CH, 128), CH)
+                low, high = restore(rbq[slot, m, :, cols], rba[slot, k, m, 0:1, :])
+                out[0:hp, there] += low
+                out[hp:per, there] += high
+                dego[:, there] += rba[slot, k, m, 1:2, :]
+
+    def scatter_copies(m):
+        made = []
+        for d in (3, 1, 2):
+            made += [copy(rsq.at[d, m], rbufq.at[d, m ^ d], s_rs.at[d, m, 0], r_rs.at[d, m ^ d, 0], rowpeer(d)),
+                     copy(rsa.at[d, m], rbufa.at[d, m ^ d], s_rs.at[d, m, 1], r_rs.at[d, m ^ d, 1], rowpeer(d))]
+        return made
 
     def scatter(m):
-        for d in range(1, R):
+        made = scatter_copies(m)
+        for i, d in enumerate((3, 1, 2)):
             rows = pl.ds(pl.multiple_of(flip(r, d) * per, 8), per)
             code, top = quantize(macc[m, rows, :])
             rsq[d, m] = code
             rsa[d, m] = top
-            send(rsq.at[d, m], rbufq.at[d, m ^ d], s_rs.at[d, m, 0], r_rs.at[d, m ^ d, 0], rowpeer(d))
-            send(rsa.at[d, m], rbufa.at[d, m ^ d], s_rs.at[d, m, 1], r_rs.at[d, m ^ d, 1], rowpeer(d))
+            made[2 * i].start()
+            made[2 * i + 1].start()
 
     early, late = p >= 1, p <= 2
+    mid = early & late
+    hp = per // 2
 
     panel_col(0)
     own(0)
@@ -580,67 +609,82 @@
     for d in (1, 2):
         direct(d, 2)
         direct(d, 3)
-    zrelay(0, (0, 1))
+    zrelay(0, range(R))
+
+    @pl.when(p == 1)
+    def _():
+        prepare(0, range(R))
+
+    @pl.when(p >= 2)
+    def _():
+        prepare(0, ())
+
+    @pl.when(early)
+    def _():
+        crosses(0, 0, 1)
     gathered(1)
+    relay(2)
     panel_col(1)
     own(1)
-    relay(2)
-    zrelay(0, (2, 3))
+
+    @pl.when(early)
+    def _():
+        cross(0, 0, 1)
+    relay(3)
     zrelay(1, (0, 1))
 
+    @pl.when(early)
+    def _():
+        cross(0, 1, 1)
+    zrelay(1, (2, 3))
+
     @pl.when(p == 1)
     def _():
-        prepare(0, range(R))
-
-    @pl.when(p >= 2)
-    def _():
-        prepare(0, ())
+        prepare(1, range(R))
+
+    @pl.when(p == 2)
+    def _():
+        prepare(1, ())
+
+    @pl.when(mid)
+    def _():
+        crosses(1, 0, 2)
 
     @pl.when(early)
     def _():
-        crosses(0, 0, 2)
-    relay(3)
+        scatter(0)
+        scatter(1)
     gathered(2)
     panel_col(2)
-    own(2)
-    zrelay(1, (2, 3))
-
-    @pl.when(early)
-    def _():
-        crosses(0, 2, 3)
     gathered(3)
     panel_col(3)
-    own(3)
 
     @pl.when(early)
     def _():
-        crosses(0, 3, 4)
         for k in range(2):
+            lax.fori_loop(2, R, lambda m, _: (cross(0, k, m), 0)[1], 0)
             give_back(0, k)
 
-    @pl.when(p == 1)
-    def _():
-        prepare(1, range(R))
-
-    @pl.when((p == 0) | (p == 2))
+    @pl.when(mid)
+    def _():
+        for k in range(2):
+            lax.fori_loop(2, R, lambda m, _: (cross(1, k, m), 0)[1], 0)
+            give_back(1, k)
+    lax.fori_loop(2, R, lambda m, _: (own(m), 0)[1], 0)
+
+    @pl.when(early)
+    def _():
+        scatter(2)
+        scatter(3)
+
+    @pl.when(p == 0)
     def _():
         prepare(1, ())
-
-    for k in range(2):
-        @pl.when(late)
-        def _():
-            def step(m, _):
-                cross(1, k, m)
-                return 0
-            lax.fori_loop(0, R, step, 0)
+        for m in range(R):
+            crosses(1, m, m + 1)
+            scatter(m)
+        for k in range(2):
             give_back(1, k)
-    for m in range(1, R):
-        scatter(m)
-    take_back(0)
-
-    @pl.when((p == 0) | (p == 3))
-    def _():
-        take_back(1)
 
     zs = zcol[0].astype(F32)
     self_term = power_eight(jnp.sum(zs * zs, axis=0, keepdims=True))
@@ -649,11 +693,9 @@
     degb[0] = degb[0] - self_term.astype(BF16).astype(F32)
     for d in range(1, R):
         send(degb, degr.at[d], s_dg.at[d], r_dg.at[d], rowpeer(d))
-    scatter(0)
-
-    hp = per // 2
+
     mine = pl.multiple_of(r * per, 8)
-    for m in (1, 2, 3, 0):
+    for m in range(R):
         for q in range(2):
             acc = macc[m, pl.ds(mine + q * hp, hp), :]
             for d in range(1, R):
@@ -669,9 +711,17 @@
         for d in range(1, R):
             total = total + degr[d, m ^ d]
         dego[:, at(m)] = total
+    take_back(0)
+
+    @pl.when((p == 0) | (p == 3))
+    def _():
+        take_back(1)
 
     for cp in started:
         cp.wait_send()
+    for m in range(R):
+        for cp in scatter_copies(m):
+            cp.wait_send()
 
     @pl.when(p == 1)
     def _():
@@ -682,13 +732,13 @@
     @pl.when(early)
     def _():
         for k in range(2):
-            for cp in retcopy(0, k):
+            for cp in back_copies(0, k):
                 cp.wait_send()
 
     @pl.when(late)
     def _():
         for k in range(2):
-            for cp in retcopy(1, k):
+            for cp in back_copies(1, k):
                 cp.wait_send()
 
 
@@ -722,10 +772,10 @@
             V((2, W + 16, slab), BF16),
             V((R, W + 16, slab), F32),
             V((2, W + 16, slab), F32),
-            V((2, W // 2, slab), I32),
-            V((2, 2, 2, half), F32),
-            V((2, W // 2, slab), I32),
-            V((2, 2, 2, half), F32),
+            V((2, R, W // R // 2, slab), I32),
+            V((2, 2, R, 2, half), F32),
+            V((2, R, W // R // 2, slab), I32),
+            V((2, 2, R, 2, half), F32),
             V((R, R, W // R // 2, slab), I32),
             V((R, R, 1, slab), F32),
             V((R, R, W // R // 2, slab), I32),
@@ -736,7 +786,7 @@
             dma((R, R, 2)), dma((R, R, 2)), dma((R, R)),
             dma((R,)), dma((2, R)), dma((2, R)),
             dma((C,)), dma((C,)), dma((R,)), dma((R,)),
-            dma((2, 2, 2)), dma((2, 2, 2)),
+            dma((2, 2, R, 2)), dma((2, 2, R, 2)),
             dma((R, R, 2)), dma((R, R, 2)),
             dma((R,)), dma((R,)),
         ],

time: 118 us -> 109 us (0.924)
  the two profiles are of different devices: /device:TPU:13 before, /device:TPU:0 now
where the time goes in v2:
time: 109 us; the launch traced here: 108 us
  Pallas kernels  104 us (95%)
  local copies, waits for them, and re-layouts  3.59 us (3%)
    pallas_call x1, Pallas kernels, folded(): pl.pallas_call(functools.partial(folded_kernel, 1e-06), out_shape=(jax.Sh...  104 us
    unnamed x2, local copies, waits for them, and re-layouts  3.59 us

profile of v2, /device:TPU:0, one launch (start us, length us, event | category | flops | bytes accessed | tf_op | source)
XLA Modules:
  0.0 108.5 jit_solution(3250382098259846753)
XLA Ops:
  0.6 104.3 %shard_map.41 = (f32[64,4096]{1,0:T(8,128)}, f32[1,4096]{1,0:T(1,128)}) custom-call(f32[150,4096]{1,0:T(8,128)} %expr.1, s32[1,256]{1,0:T(1,128)} %bitcast.3), custom_call_target="tpu_custom_call" | custom-call | tf_op jit(solution)/shard_map/pallas_call | solution.py:756
  104.9 2.3 %copy.6 = f32[64,4096]{1,0:T(8,128)} copy(f32[64,4096]{1,0:T(8,128)} %get-tuple-element.8) | data formatting | bytes 2097152
  107.2 1.3 %copy.7 = f32[4096]{0:T(1024)} copy(f32[4096]{0:T(1024)} %bitcast.2) | data formatting | bytes 32768

commit v3 on v2

--- a/solution.py
+++ b/solution.py
@@ -461,9 +461,15 @@
     zslot = p // 3
     zpeer = colpeer(jnp.where(p == 3, 1, p + 1))
 
-    def zsend(d):
+    def zsend_copy(d):
         rows = block(d)
-        send(zcol.at[0, rows, :], zf.at[zslot, rows, :], s_z.at[d], r_z.at[zslot, d], zpeer)
+        return copy(zcol.at[0, rows, :], zf.at[zslot, rows, :], s_z.at[d], r_z.at[zslot, d], zpeer)
+
+    def zsend(ds, cond):
+        @pl.when(cond)
+        def _():
+            for d in ds:
+                zsend_copy(d).start()
 
     pick = jnp.zeros((pad, W), F32)
     for m in range(R):
@@ -473,7 +479,7 @@
     zw[0] = pick.astype(BF16)
     for d in range(1, C):
         send(zw.at[0], zw.at[d], s_zc.at[d], r_zc.at[d], {"col": lax.rem(c + d, C)})
-    zsend(0)
+    zsend((0,), p >= 0)
 
     relay(0)
     tot = zw[0].astype(F32)
@@ -488,7 +494,7 @@
     for d in range(1, R):
         for e in range(2):
             landed(d, 0, e)
-        zsend(d)
+        zsend((d,), p < 3)
 
     zt[0] = zcol[0].T
     for d in range(1, R):
@@ -523,32 +529,31 @@
             return 0
         lax.fori_loop(0, 2 * (m_hi - m_lo), step, 0)
 
-    def prepare(f, known):
-        for d in range(R):
-            if d not in known:
-                arrived(zf.at[f, block(d), :], r_z.at[f, d])
+    def prepare(f):
         zt[1 + f] = zf[f].T
         prow[f, 0:W, :] = power_eight(dot(zwn[...], zf[f])).astype(BF16)
 
-    def zcopy(f, d):
+    def zwait(f, ds):
+        for d in ds:
+            arrived(zf.at[f, block(d), :], r_z.at[f, d])
+
+    def zrelay_copy(f, d):
         rows = block(d)
-        dest = 2 if f == 0 else 0
-        return copy(zf.at[f, rows, :], zf.at[1, rows, :], s_zf.at[f, d], r_z.at[1, d], colpeer(dest))
+        return copy(zf.at[f, rows, :], zf.at[1, rows, :], s_zf.at[f, d], r_z.at[1, d], colpeer(2 + f))
 
     def zrelay(f, ds):
-        @pl.when(p == 1)
+        @pl.when(p == 1 + f)
         def _():
             for d in ds:
-                arrived(zf.at[f, block(d), :], r_z.at[f, d])
-                zcopy(f, d).start()
+                zwait(f, (d,))
+                zrelay_copy(f, d).start()
 
     def back_copies(f, k):
         cols = slice(k * CH, (k + 1) * CH)
         if f == 0:
             dest, slot = p - 1, 0
         else:
-            dest = jnp.where(p == 2, 0, 3)
-            slot = (p + 1) // 2
+            dest, slot = jnp.where(p == 1, 3, 0), p - 1
         made = []
         for d in (3, 1, 2, 0):
             dev = {**colpeer(dest), **(rowpeer(d) if d else {})}
@@ -599,8 +604,7 @@
             made[2 * i].start()
             made[2 * i + 1].start()
 
-    early, late = p >= 1, p <= 2
-    mid = early & late
+    away = p >= 1
     hp = per // 2
 
     panel_col(0)
@@ -611,80 +615,59 @@
         direct(d, 3)
     zrelay(0, range(R))
 
-    @pl.when(p == 1)
-    def _():
-        prepare(0, range(R))
-
     @pl.when(p >= 2)
     def _():
-        prepare(0, ())
-
-    @pl.when(early)
+        zwait(0, range(R))
+
+    @pl.when(away)
     def _():
+        prepare(0)
         crosses(0, 0, 1)
     gathered(1)
     relay(2)
     panel_col(1)
     own(1)
-
-    @pl.when(early)
+    relay(3)
+    zsend((1, 2, 3), p == 3)
+    zrelay(1, (0,))
+
+    @pl.when(away)
     def _():
-        cross(0, 0, 1)
-    relay(3)
-    zrelay(1, (0, 1))
-
-    @pl.when(early)
-    def _():
-        cross(0, 1, 1)
-    zrelay(1, (2, 3))
-
-    @pl.when(p == 1)
-    def _():
-        prepare(1, range(R))
-
-    @pl.when(p == 2)
-    def _():
-        prepare(1, ())
-
-    @pl.when(mid)
-    def _():
-        crosses(1, 0, 2)
-
-    @pl.when(early)
-    def _():
-        scatter(0)
-        scatter(1)
+        crosses(0, 1, 2)
+    zrelay(1, (1, 2))
     gathered(2)
     panel_col(2)
     gathered(3)
     panel_col(3)
-
-    @pl.when(early)
-    def _():
-        for k in range(2):
+    for k in range(2):
+        @pl.when(away)
+        def _():
             lax.fori_loop(2, R, lambda m, _: (cross(0, k, m), 0)[1], 0)
             give_back(0, k)
-
-    @pl.when(mid)
+        if k == 0:
+            zrelay(1, (3,))
+
+    @pl.when((p == 1) | (p == 3))
+    def _():
+        zwait(1, range(R))
+
+    @pl.when(away)
+    def _():
+        prepare(1)
+    for m in range(2):
+        @pl.when(away)
+        def _():
+            crosses(1, m, m + 1)
+        scatter(m)
+
+    @pl.when(away)
     def _():
         for k in range(2):
             lax.fori_loop(2, R, lambda m, _: (cross(1, k, m), 0)[1], 0)
             give_back(1, k)
-    lax.fori_loop(2, R, lambda m, _: (own(m), 0)[1], 0)
-
-    @pl.when(early)
-    def _():
-        scatter(2)
-        scatter(3)
-
-    @pl.when(p == 0)
-    def _():
-        prepare(1, ())
-        for m in range(R):
-            crosses(1, m, m + 1)
-            scatter(m)
-        for k in range(2):
-            give_back(1, k)
+    for m in range(2, R):
+        own(m)
+        scatter(m)
 
     zs = zcol[0].astype(F32)
     self_term = power_eight(jnp.sum(zs * zs, axis=0, keepdims=True))
@@ -713,9 +696,10 @@
         dego[:, at(m)] = total
     take_back(0)
 
-    @pl.when((p == 0) | (p == 3))
+    @pl.when(p == 0)
     def _():
         take_back(1)
+        take_back(2)
 
     for cp in started:
         cp.wait_send()
@@ -723,23 +707,21 @@
         for cp in scatter_copies(m):
             cp.wait_send()
 
-    @pl.when(p == 1)
+    for d in range(R):
+        zsend_copy(d).wait_send()
+
+    for f in range(2):
+        @pl.when(p == 1 + f)
+        def _():
+            for d in range(R):
+                zrelay_copy(f, d).wait_send()
+
+    @pl.when(away)
     def _():
         for f in range(2):
-            for d in range(R):
-                zcopy(f, d).wait_send()
-
-    @pl.when(early)
-    def _():
-        for k in range(2):
-            for cp in back_copies(0, k):
-                cp.wait_send()
-
-    @pl.when(late)
-    def _():
-        for k in range(2):
-            for cp in back_copies(1, k):
-                cp.wait_send()
+            for k in range(2):
+                for cp in back_copies(f, k):
+                    cp.wait_send()
 
 
 def folded(expr, win):
@@ -774,8 +756,8 @@
             V((2, W + 16, slab), F32),
             V((2, R, W // R // 2, slab), I32),
             V((2, 2, R, 2, half), F32),
-            V((2, R, W // R // 2, slab), I32),
-            V((2, 2, R, 2, half), F32),
+            V((3, R, W // R // 2, slab), I32),
+            V((3, 2, R, 2, half), F32),
             V((R, R, W // R // 2, slab), I32),
             V((R, R, 1, slab), F32),
             V((R, R, W // R // 2, slab), I32),
@@ -786,12 +768,12 @@
             dma((R, R, 2)), dma((R, R, 2)), dma((R, R)),
             dma((R,)), dma((2, R)), dma((2, R)),
             dma((C,)), dma((C,)), dma((R,)), dma((R,)),
-            dma((2, 2, R, 2)), dma((2, 2, R, 2)),
+            dma((2, 2, R, 2)), dma((3, 2, R, 2)),
             dma((R, R, 2)), dma((R, R, 2)),
             dma((R,)), dma((R,)),
         ],
         compiler_params=pltpu.CompilerParams(
-            collective_id=0, has_side_effects=True, vmem_limit_bytes=60 << 20),
+            collective_id=0, has_side_effects=True, vmem_limit_bytes=46 << 20),
     )(expr, win.reshape(1, W))
     return margin, degree.reshape(width)
 

time: 109 us -> 102 us (0.936)
  the two profiles are of different devices: /device:TPU:0 before, /device:TPU:1 now
where the time goes in v3:
time: 102 us
  Pallas kernels  97 us (95%)
  local copies, waits for them, and re-layouts  3.95 us (4%)
    pallas_call x1, Pallas kernels, folded(): pl.pallas_call(functools.partial(folded_kernel, 1e-06), out_shape=(jax.Sh...  97 us
    unnamed x6, local copies, waits for them, and re-layouts  3.95 us

profile of v3, /device:TPU:1, one launch (start us, length us, event | category | flops | bytes accessed | tf_op | source)
XLA Modules:
  0.0 101.6 jit_solution(23941637308277306)
XLA Ops:
  0.6 0.0 copy-start
  0.6 1.7 %copy-done = f32[150,4096]{1,0:T(8,128)S(1)} copy-done((f32[150,4096]{1,0:T(8,128)S(1)}, f32[150,4096]{1,0:T(8,128)}, u32[]{:S(2)}) %copy-start) | copy-done | bytes 2457624
  2.3 0.0 copy-start.1
  2.3 0.7 copy-done.1
  3.0 97.0 %shard_map.41 = (f32[64,4096]{1,0:T(8,128)S(1)}, f32[1,4096]{1,0:T(1,128)S(1)}) custom-call(f32[150,4096]{1,0:T(8,128)S(1)} %copy-done, s32[1,256]{1,0:T(1,128)S(1)} %bitcast.3), custom_call_target="tpu_custom_call" | custom-call | tf_op jit(solution)/shard_map/pallas_call | solution.py:738
  100.0 1.0 copy.6
  100.9 0.6 copy.7
Async XLA Ops:
  0.6 1.7 %copy-start = (f32[150,4096]{1,0:T(8,128)S(1)}, f32[150,4096]{1,0:T(8,128)}, u32[]{:S(2)}) copy-start(f32[150,4096]{1,0:T(8,128)} %expr.1) | copy-start | bytes 7372804
  2.3 0.7 copy-start.1

commit v4 on v3

--- a/solution.py
+++ b/solution.py
@@ -628,7 +628,6 @@
     panel_col(1)
     own(1)
     relay(3)
-    zsend((1, 2, 3), p == 3)
     zrelay(1, (0,))
 
     @pl.when(away)
@@ -636,7 +635,10 @@
         crosses(0, 1, 2)
     zrelay(1, (1, 2))
     gathered(2)
+    zsend((1, 2, 3), p == 3)
     panel_col(2)
+    zrelay(1, (3,))
+    own(2)
     gathered(3)
     panel_col(3)
     for k in range(2):
@@ -644,8 +646,6 @@
         def _():
             lax.fori_loop(2, R, lambda m, _: (cross(0, k, m), 0)[1], 0)
             give_back(0, k)
-        if k == 0:
-            zrelay(1, (3,))
 
     @pl.when((p == 1) | (p == 3))
     def _():
@@ -665,9 +665,9 @@
         for k in range(2):
             lax.fori_loop(2, R, lambda m, _: (cross(1, k, m), 0)[1], 0)
             give_back(1, k)
-    for m in range(2, R):
-        own(m)
-        scatter(m)
+    scatter(2)
+    own(3)
+    scatter(3)
 
     zs = zcol[0].astype(F32)
     self_term = power_eight(jnp.sum(zs * zs, axis=0, keepdims=True))

time: 102 us -> 103 us (level)
  Pallas kernels: 97 us -> 98.1 us
    pallas_call x1, Pallas kernels: 97 us -> 98.1 us  [folded(): pl.pallas_call(functools.partial(folded_kernel, 1e-06), out_shape=(jax.Sh...]
where the time goes in v4:
time: 103 us
  Pallas kernels  98.1 us (95%)
  local copies, waits for them, and re-layouts  3.95 us (4%)
    pallas_call x1, Pallas kernels, folded(): pl.pallas_call(functools.partial(folded_kernel, 1e-06), out_shape=(jax.Sh...  98.1 us
    unnamed x6, local copies, waits for them, and re-layouts  3.95 us

profile of v4, /device:TPU:1, one launch (start us, length us, event | category | flops | bytes accessed | tf_op | source)
XLA Modules:
  0.0 102.7 jit_solution(16555449028946957224)
XLA Ops:
  0.6 0.0 copy-start
  0.6 1.7 %copy-done = f32[150,4096]{1,0:T(8,128)S(1)} copy-done((f32[150,4096]{1,0:T(8,128)S(1)}, f32[150,4096]{1,0:T(8,128)}, u32[]{:S(2)}) %copy-start) | copy-done | bytes 2457624
  2.3 0.0 copy-start.1
  2.3 0.7 copy-done.1
  3.0 98.1 %shard_map.41 = (f32[64,4096]{1,0:T(8,128)S(1)}, f32[1,4096]{1,0:T(1,128)S(1)}) custom-call(f32[150,4096]{1,0:T(8,128)S(1)} %copy-done, s32[1,256]{1,0:T(1,128)S(1)} %bitcast.3), custom_call_target="tpu_custom_call" | custom-call | tf_op jit(solution)/shard_map/pallas_call | solution.py:738
  101.1 1.0 copy.6
  102.1 0.6 copy.7
Async XLA Ops:
  0.6 1.7 %copy-start = (f32[150,4096]{1,0:T(8,128)S(1)}, f32[150,4096]{1,0:T(8,128)}, u32[]{:S(2)}) copy-start(f32[150,4096]{1,0:T(8,128)} %expr.1) | copy-start | bytes 7372804
  2.3 0.7 copy-start.1
